TPU v7x, 32 devices: a whole 2x2x4 slice. The times are simulated.
32 devices in a mesh: rows: 16 (over z, x, core), inner: 2 (over y).
Axes of the slice: x: 2, y: 2, z: 4, core: 2. Of those that a mesh axis runs over, the one named last changes fastest.
Arguments:
- blocks: bfloat16 [16, 16, 256, 256], P('rows'), may hold values from -0.375 to 0.375
- columns: int32 [16, 16], replicated, may hold values from -1 to 15, as said below
Outputs:
- purified: float32 [16, 16, 256, 256], P('rows', None, 'inner')
Inputs may be any that keep to these rules, and one draw needn't show every extreme that they name: Each entry of row i that is not -1 is (i + d) mod 16 for an offset d with -16 <= 2 * d < 16; the entries of a row are distinct and stand before its -1 entries; every row lists its diagonal block; some row lists 16 columns.
All inputs are finite; a program needn't handle non-finite values.
Results may differ from a plain program's by a relative error of at most 0.0055.
Values may be sent and summed in bfloat16 or wider, within the bound.
A program may use at most 128 MiB of HBM per device.

v0:
```python
import functools

import jax
import jax.numpy as jnp
from jax import lax
from jax.experimental import pallas as pl
from jax.experimental.pallas import tpu as pltpu
from jax.sharding import PartitionSpec as P

MESH = pl.DeviceIdType.MESH

def grid_kernel(columns, raw, out, own, other, lane_live, panels, acc, pure, final, load_sem,
                left_send, left_recv, pass_send, pass_recv, panel_send, panel_recv, end_send, end_recv):
    residues, depth, block, _ = own.shape
    band = residues * depth
    slab = block // 2
    width = depth * slab
    rank, y = lax.axis_index("rows"), lax.axis_index("inner")
    rows = lax.axis_size("rows")
    core, x, z = rank % 2, (rank // 2) % 2, rank // 4
    upper, low = z // 2, z % 2
    to_core, to_x, to_z = 1 - 2 * core, 1 - 2 * x, 1 - 2 * low
    far_rank = lax.rem(rank + rows // 2, rows)
    at_far = {"rows": far_rank, "inner": y}
    at_y = {"rows": rank, "inner": 1 - y}
    at_far_y = {"rows": far_rank, "inner": 1 - y}
    at_z = {"rows": rank + 4 * to_z, "inner": y}
    at_x = {"rows": rank + 2 * to_x, "inner": y}
    at_core = {"rows": rank + to_core, "inner": y}
    everyone = (at_far, at_y, at_far_y, at_z, at_x, at_core)

    barrier = pltpu.get_barrier_semaphore()
    for device in everyone:
        pl.semaphore_signal(barrier, inc=1, device_id=device, device_id_type=MESH)

    here = pl.ds(pl.multiple_of(y * slab, slab), slab)
    there = pl.ds(pl.multiple_of((1 - y) * slab, slab), slab)
    loads = [pltpu.make_async_copy(raw.at[:, which], own.at[which], load_sem.at[which]) for which in range(residues)]
    for load in loads:
        load.start()
    sent = []
    classes = (0, 1)

    def residue(side, q, x_at, core_at):
        return (side + 2 * q + 2 * residues - 2 * x_at - core_at) % residues

    mine = [residue(upper, q, x, core) for q in classes]
    fars = [residue(1 - upper, q, x, core) for q in classes]

    def is_live(row_at, slot):
        target = (row_at + slot + rows - band // 2) % rows
        found = columns[row_at, 0] == target
        for at in range(1, columns.shape[1]):
            found = found | (columns[row_at, at] == target)
        return jnp.where(found, 1, 0)

    def remote(source, target, send_sem, recv_sem, device):
        return pltpu.make_async_remote_copy(
            src_ref=source, dst_ref=target, send_sem=send_sem, recv_sem=recv_sem, device_id=device, device_id_type=MESH
        )

    def go(copy):
        copy.start()
        sent.append(copy)

    def send_left(number):
        which = (fars + mine)[number]
        go(remote(own.at[which, :, :, here], other.at[which, :, :, here],
                  left_send.at[number], left_recv.at[number], at_far))

    def pass_left(number):
        ref = other.at[(mine + fars)[number], :, :, here]
        remote(ref, ref, left_send.at[number], left_recv.at[number], at_far).wait_recv()
        go(remote(ref, ref, pass_send.at[number], pass_recv.at[number], at_y))

    def end_left(number):
        ref = other.at[(mine + fars)[number], :, :, there]
        remote(ref, ref, pass_send.at[number], pass_recv.at[number], at_y).wait_recv()

    def send_panel(product, q, source, target, send_at, device):
        go(remote(panels.at[product, q, source], panels.at[product, q, target],
                  panel_send.at[product, q, send_at], panel_recv.at[product, q, target], device))

    def share(product, q, source):
        send_panel(product, q, source, 8 + source, 8 + source, at_core)

    def take(product, q, source):
        ref = panels.at[product, q, source]
        remote(ref, ref, panel_send.at[product, q, 0], panel_recv.at[product, q, source], at_core).wait_recv()
        if source < 8:
            share(product, q, source)

    def spread(product, q, row):
        send_panel(product, q, row, 2 + row, row, at_z)
        send_panel(product, q, row, 4 + row, 2 + row, at_x)
        share(product, q, row)

    def mac(product, q, source, row, left):
        chip_core, chip, far = source // 8, (source // 2) % 4, source % 2
        delta = 4 * (to_z * (chip % 2) + 2 * far - 2 * row) + 2 * to_x * (chip // 2) + to_core * chip_core
        slot = (delta + band // 2 + 2 * rows) % rows
        theirs = residue(upper, q, x + to_x * (chip // 2), core + to_core * chip_core)
        shift = (theirs - mine[q] + slot) // residues
        block_left = left[slot % residues, slot // residues]
        tile = 2 * slab
        for part in range(width // tile):
            lanes = pl.ds(pl.multiple_of(shift * slab + part * tile, slab), tile)
            acc[row, q, :, lanes] += jnp.dot(
                block_left, panels[product, q, source, :, part * tile : (part + 1) * tile],
                preferred_element_type=jnp.float32,
            )

    middle = slice(depth // 2 * slab, depth // 2 * slab + width)

    def masked_total(row, q):
        keep = lane_live[row : row + 1, q * width : (q + 1) * width] > 0
        return jnp.where(keep, acc[row, q, :, middle], 0.0)

    acc[...] = jnp.zeros_like(acc)
    for row, row_at in enumerate((rank, far_rank)):
        for q in classes:
            for w in range(depth):
                first = q * width + w * slab
                live = is_live(row_at, residues * w + mine[q])
                lane_live[row : row + 1, first : first + slab] = jnp.full((1, slab), live)

    def mask_slot(slot, carry):
        which, w = slot % residues, slot // residues
        keep = jnp.full((1, block), is_live(rank, slot)) > 0
        value = own[which, w]
        own[which, w] = jnp.where(keep, value, jnp.zeros_like(value))
        return carry

    def fill(q, row, left):
        for w in range(depth):
            panels[0, q, row, :, w * slab : (w + 1) * slab] = left[mine[q], w, :, here]

    for load in loads:
        load.wait()
    lax.fori_loop(0, band, mask_slot, 0)
    for q in classes:
        fill(q, 0, own)
    pl.semaphore_wait(barrier, len(everyone))

    for q in classes:
        send_left(q)
        spread(0, q, 0)

    def own_macs(q, first, gap, count):
        def body(n, carry):
            mac(0, q, first + gap * n, 0, own)
            return carry

        lax.fori_loop(0, count, body, 0)

    def both_own_macs(first, gap, count):
        def body(n, carry):
            for q in classes:
                mac(0, q, first + gap * n, 0, own)
            return carry

        lax.fori_loop(0, count, body, 0)

    both_own_macs(0, 1, 1)
    for q in classes:
        take(0, q, 2)
        send_panel(0, q, 2, 6, 4, at_x)
        take(0, q, 4)
        pass_left(q)
        fill(q, 1, other)
        spread(0, q, 1)
    send_left(2)
    send_left(3)
    for q in classes:
        for source in (8, 9, 10, 12):
            take(0, q, source)
    both_own_macs(1, 1, 2)
    both_own_macs(8, 1, 3)
    take(0, 0, 6)
    for q in classes:
        take(0, q, 3)
        send_panel(0, q, 3, 7, 5, at_x)
        take(0, q, 5)
    take(0, 1, 6)
    both_own_macs(3, 1, 4)
    for q in classes:
        for source in (11, 13, 14):
            take(0, q, source)
    both_own_macs(11, 1, 4)
    pass_left(2)
    pass_left(3)

    def second_row(q):
        def body(source, carry):
            mac(0, q, source, 1, other)
            return carry

        lax.fori_loop(0, rows, body, 0)

    def square(row, q):
        panels[1, q, row] = masked_total(row, q).astype(panels.dtype)
        acc[row, q] = jnp.zeros_like(acc[row, q])

    def last_own(q):
        take(0, q, 7)
        take(0, q, 15)
        own_macs(q, 7, 8, 2)
        square(0, q)

    def pair_macs(q, first, gap, count):
        def body(n, carry):
            mac(1, q, first + gap * n, 0, own)
            mac(1, q, first + gap * n, 1, other)
            return carry

        lax.fori_loop(0, count, body, 0)

    last_own(0)
    spread(1, 0, 0)
    for number in range(residues):
        end_left(number)
    second_row(0)
    square(1, 0)
    spread(1, 0, 1)
    last_own(1)
    take(1, 0, 2)
    send_panel(1, 0, 2, 6, 4, at_x)
    spread(1, 1, 0)
    second_row(1)
    square(1, 1)
    take(1, 0, 4)
    take(1, 0, 8)
    take(1, 0, 9)
    take(1, 0, 5)
    send_panel(1, 0, 5, 7, 5, at_z)
    spread(1, 1, 1)

    def finish(q):
        for row in (1, 0):
            total = 3.0 * panels[1, q, row].astype(jnp.float32) - 2.0 * masked_total(row, q)
            pure[row, q] = total.astype(pure.dtype)
            if row == 1:
                go(remote(pure.at[1, q, here], final.at[1, q], end_send.at[1, q], end_recv.at[1, q], at_far))
                go(remote(pure.at[1, q, there], final.at[2, q], end_send.at[2, q], end_recv.at[2, q], at_far_y))
        go(remote(pure.at[0, q, there], final.at[0, q], end_send.at[0, q], end_recv.at[0, q], at_y))

    pair_macs(0, 0, 1, 2)
    pair_macs(0, 8, 1, 2)
    pair_macs(0, 2, 2, 2)
    take(1, 0, 3)
    take(1, 0, 10)
    take(1, 0, 12)
    pair_macs(0, 3, 2, 2)
    pair_macs(0, 10, 2, 2)
    take(1, 1, 2)
    send_panel(1, 1, 2, 6, 4, at_x)
    take(1, 0, 6)
    take(1, 0, 7)
    pair_macs(0, 6, 1, 2)
    for source in (11, 13, 14, 15):
        take(1, 0, source)
    pair_macs(0, 11, 2, 2)
    pair_macs(0, 14, 1, 2)
    finish(0)
    take(1, 1, 4)
    take(1, 1, 5)
    send_panel(1, 1, 5, 7, 5, at_z)
    take(1, 1, 3)
    for source in (8, 9, 10, 12):
        take(1, 1, source)
    pair_macs(1, 0, 1, 6)
    pair_macs(1, 8, 1, 3)
    take(1, 1, 11)
    take(1, 1, 13)
    pair_macs(1, 11, 1, 3)
    for source in (6, 7, 14, 15):
        take(1, 1, source)
    pair_macs(1, 6, 1, 2)
    pair_macs(1, 14, 1, 2)
    finish(1)

    def place(value, which, side):
        for w in range(depth):
            out[residues * w + which, :, side] = value[:, w * slab : (w + 1) * slab]

    for q in classes:
        place(pure[0, q, here], mine[q], here)
    for q in classes:
        for number, which, side in ((0, mine[q], there), (1, fars[q], here), (2, fars[q], there)):
            ref = final.at[number, q]
            remote(ref, ref, end_send.at[number, q], end_recv.at[number, q], at_y).wait_recv()
            place(final[number, q], which, side)
    for copy in sent:
        copy.wait_send()


def on_grid(blocks, columns):
    _, band_width, block_size, _ = blocks.shape
    rows = lax.axis_size("rows")
    residues = 4
    depth, slab = band_width // residues, block_size // 2
    width = depth * slab
    raw = blocks.reshape(depth, residues, block_size, block_size)
    vmem = pl.BlockSpec(memory_space=pltpu.VMEM)
    dma = pltpu.SemaphoreType.DMA
    result = pl.pallas_call(
        grid_kernel,
        out_shape=jax.ShapeDtypeStruct((band_width, slab, block_size), blocks.dtype),
        in_specs=[pl.BlockSpec(memory_space=pltpu.SMEM), pl.BlockSpec(memory_space=pl.ANY)],
        out_specs=vmem,
        scratch_shapes=[
            pltpu.VMEM((residues, depth, block_size, block_size), blocks.dtype),
            pltpu.VMEM((residues, depth, block_size, block_size), blocks.dtype),
            pltpu.VMEM((2, 2 * width), jnp.int32),
            pltpu.VMEM((2, 2, rows, block_size, width), blocks.dtype),
            pltpu.VMEM((2, 2, block_size, 2 * width), jnp.float32),
            pltpu.VMEM((2, 2, block_size, width), blocks.dtype),
            pltpu.VMEM((3, 2, slab, width), blocks.dtype),
            dma((4,)), dma((4,)), dma((4,)), dma((4,)), dma((4,)),
            dma((2, 2, 16)), dma((2, 2, 16)), dma((3, 2)), dma((3, 2)),
        ],
        compiler_params=pltpu.CompilerParams(
            collective_id=0, has_side_effects=True, vmem_limit_bytes=60 * 1024 * 1024
        ),
    )(columns, raw)
    return result[None].astype(jnp.float32)


def from_behind(value, axis, steps):
    count = lax.axis_size(axis)
    pairs = [(source, (source + steps) % count) for source in range(count)]
    return lax.ppermute(value, axis, pairs)


def live_table(columns):
    nrows, band_width = columns.shape
    half_band = band_width // 2
    row_ids = jnp.arange(nrows, dtype=jnp.int32)
    target = (
        row_ids[:, None] + jnp.arange(band_width, dtype=jnp.int32)[None, :] - half_band
    ) % nrows
    return jnp.any(columns[:, None, :] == target[:, :, None], axis=2)


def slot_shift(piece, delta):
    band_width = piece.shape[1]
    if delta >= 0:
        return jnp.concatenate([piece[:, delta:], jnp.zeros_like(piece[:, :delta])], axis=1)
    return jnp.concatenate(
        [jnp.zeros_like(piece[:, :-delta]), piece[:, : band_width + delta]], axis=1
    )


def fetch_band(row_slab, below, above, block_rows, second):
    band_width = row_slab.shape[1]
    pieces = []
    for offset in range(-below, above + 1):
        if offset == 0:
            pieces.append(row_slab)
            continue
        trimmed = (abs(offset) - 1) * block_rows + 1
        if offset > 0:
            outgoing = row_slab[:, : band_width - trimmed]
        else:
            outgoing = row_slab[:, trimmed:]
        if second:
            incoming = from_behind(outgoing, "rows", -offset)
        else:
            incoming = from_behind(outgoing, "rows", -offset)
        filler = jnp.zeros_like(row_slab[:, :trimmed])
        if offset > 0:
            pieces.append(jnp.concatenate([incoming, filler], axis=1))
        else:
            pieces.append(jnp.concatenate([filler, incoming], axis=1))
    return jnp.concatenate(pieces, axis=0)


def merge_groups(totals):
    rounded = lax.optimization_barrier(totals.astype(jnp.bfloat16))
    return jnp.sum(rounded.astype(jnp.float32), axis=0)


def dense_terms(left, window, window_base, groups):
    block_rows, band_width, block_size, inner_width = left.shape
    out_width = window.shape[3]
    half_band = band_width // 2
    group_width = inner_width // groups
    stacked = jnp.stack(
        [
            slot_shift(
                window[window_base + offset : window_base + offset + block_rows], half_band - offset
            )
            for offset in range(band_width)
        ],
        axis=1,
    )
    left_groups = left.reshape(block_rows, band_width, block_size, groups, group_width)
    right_groups = stacked.reshape(
        block_rows, band_width, band_width, groups, group_width, out_width
    )
    totals = jnp.einsum(
        "ramcq,rascqn->crsmn", left_groups, right_groups, preferred_element_type=jnp.float32
    )
    return merge_groups(totals)


def band_terms(left, window, window_base, groups):
    return dense_terms(left, window, window_base, groups)


def per_device(blocks, columns):
    block_rows, band_width, block_size, _ = blocks.shape
    half_band = band_width // 2
    inner_count = lax.axis_size("inner")
    slab_width = block_size // inner_count
    inner_index = lax.axis_index("inner")
    row_owner = lax.axis_index("rows")
    live_own = lax.dynamic_slice_in_dim(live_table(columns), row_owner * block_rows, block_rows, 0)
    live_slots = live_own[:, :, None, None]
    masked = jnp.where(live_slots, blocks, jnp.zeros_like(blocks))
    below = -(-half_band // block_rows)
    above = -(-(half_band - 1) // block_rows)
    window_base = below * block_rows - half_band
    row_slab = lax.dynamic_slice_in_dim(masked, inner_index * slab_width, slab_width, 3)
    window = fetch_band(row_slab, below, above, block_rows, False)
    square = band_terms(masked, window, window_base, inner_count)
    square = jnp.where(live_slots, square, jnp.float32(0.0)).astype(jnp.bfloat16)
    second_window = fetch_band(square, below, above, block_rows, True)
    cubed = band_terms(masked, second_window, window_base, inner_count)
    cubed = jnp.where(live_slots, cubed, jnp.float32(0.0))
    column_slabs = 3.0 * square.astype(jnp.float32) - 2.0 * cubed
    return lax.all_to_all(
        column_slabs.astype(jnp.bfloat16), "inner", split_axis=2, concat_axis=3, tiled=True
    ).astype(column_slabs.dtype)


def solution(mesh):
    in_specs = (P("rows", None, None, None), P())
    out_specs = P("rows", None, "inner", None)

    def step(blocks, columns):
        plain = mesh.shape["rows"] == 16 and mesh.shape["inner"] == 2
        if plain and blocks.shape[:2] == (16, 16) and blocks.shape[2] % 256 == 0:
            chosen = on_grid
        else:
            chosen = per_device
        return jax.shard_map(chosen, mesh=mesh, in_specs=in_specs, out_specs=out_specs, check_vma=False)(
            blocks, columns
        )

    return step
```

profile of v0, /device:TPU:0, one launch (start us, length us, event | category | flops | bytes accessed | tf_op | source)
XLA Modules:
  0.0 126.5 jit_solution(737204378842706414)
XLA Ops:
  0.0 123.7 %shard_map.28 = bf16[16,128,256]{2,1,0:T(8,128)(2,1)} custom-call(s32[16,16]{1,0:T(8,128)} %columns.1, bf16[4,4,256,256]{3,2,1,0:T(8,128)(2,1)} %bitcast.4), custom_call_target="tpu_custom_call" | custom-call | tf_op jit(solution)/shard_map/pallas_call | solution.py:306
  123.7 2.8 %bitcast_convert_fusion = f32[1,16,128,256]{3,2,1,0:T(8,128)} fusion(bf16[16,128,256]{2,1,0:T(8,128)(2,1)} %shard_map.28), kind=kLoop, calls=%fused_computation | loop fusion | flops 524288 | bytes 3145728 | tf_op jit(solution)/shard_map/convert_element_type | solution.py:326
where the time goes:
time: 127 us
  Pallas kernels  124 us (98%)
  other arithmetic  2.77 us (2%)
    pallas_call x1, Pallas kernels, on_grid(): pl.pallas_call(grid_kernel, out_shape=jax.ShapeDtypeStruct((band_width, s...  124 us
    convert_element_type x1, other arithmetic, on_grid(): return result[None].astype(jnp.float32)  2.77 us

commit v1 on v0

v1 whole, which is shorter than its diff:
```python
import functools

import jax
import jax.numpy as jnp
from jax import lax
from jax.experimental import pallas as pl
from jax.experimental.pallas import tpu as pltpu
from jax.sharding import PartitionSpec as P

MESH = pl.DeviceIdType.MESH

WINDOW = 3
EXTRA = ((0, 0),)
GROUP = ((0, 0), (1, 0), (0, 1), (1, 1))
ORDER = (
    ("x", 1, 1, 0, 0), ("x", 1, 1, 0, 1), ("l", 1, 0, 0, 0, 0), ("l", 1, 0, 0, 0, 1), ("p", 4, 0),
("p", 4, 1), ("x", 0, 0, 0, 0), ("x", 0, 0, 0, 1), ("l", 2, 0, 1, 0, 0), ("l", 2, 0, 1, 0, 1),
("x", 1, 0, 0, 0), ("x", 1, 0, 0, 1), ("l", 1, 1, 0, 0, 0), ("l", 1, 1, 0, 0, 1), ("p", 5, 0), ("p", 5, 1),
("l", 3, 0, 0, 0, 0), ("l", 3, 0, 0, 0, 1), ("l", 2, 0, 0, 0, 0), ("l", 2, 0, 0, 0, 1),
("l", 1, 0, 1, 0, 0), ("l", 1, 0, 1, 0, 1), ("x", 0, 0, 1, 0), ("x", 0, 0, 1, 1), ("l", 1, 1, 1, 0, 0),
("l", 1, 1, 1, 0, 1), ("p", 7, 0), ("p", 7, 1), ("l", 3, 0, 1, 0, 0), ("l", 3, 0, 1, 0, 1), ("p", 6, 0),
("p", 6, 1), ("l", 2, 1, 1, 0, 0), ("l", 2, 1, 1, 0, 1), ("p", 8, 0), ("p", 8, 1), ("p", 9, 0), ("p", 9, 1),
("p", 10, 0), ("p", 10, 1), ("p", 11, 0), ("p", 11, 1), ("p", 12, 0), ("p", 12, 1), ("p", 13, 0),
("p", 13, 1), ("p", 14, 0), ("p", 14, 1), ("p", 15, 0), ("p", 15, 1), ("s", 0), ("l", 3, 1, 0, 0, 0),
("l", 3, 1, 0, 0, 1), ("l", 1, 0, 0, 1, 0), ("l", 1, 0, 0, 1, 1), ("l", 1, 1, 0, 1, 0),
("l", 1, 1, 0, 1, 1), ("l", 1, 0, 1, 1, 0), ("l", 1, 0, 1, 1, 1), ("l", 1, 1, 1, 1, 0),
("l", 1, 1, 1, 1, 1), ("s", 1), ("l", 2, 1, 0, 0, 0), ("l", 2, 1, 0, 0, 1), ("q", 4, 0), ("q", 4, 1),
("l", 3, 1, 1, 0, 0), ("l", 3, 1, 1, 0, 1), ("l", 2, 0, 1, 1, 0), ("l", 2, 0, 1, 1, 1),
("l", 2, 0, 0, 1, 0), ("l", 2, 0, 0, 1, 1), ("l", 2, 1, 1, 1, 0), ("l", 2, 1, 1, 1, 1),
("l", 2, 1, 0, 1, 0), ("l", 2, 1, 0, 1, 1), ("s", 2), ("q", 5, 0), ("q", 5, 1), ("l", 3, 0, 0, 1, 0),
("l", 3, 0, 0, 1, 1), ("l", 3, 0, 1, 1, 0), ("l", 3, 0, 1, 1, 1), ("l", 3, 1, 0, 1, 0),
("l", 3, 1, 0, 1, 1), ("l", 3, 1, 1, 1, 0), ("l", 3, 1, 1, 1, 1), ("s", 3), ("c", 0, 1), ("c", 2, 3),
("c", 4, 5), ("c", 8, 9), ("c", 12, 13), ("q", 6, 0), ("q", 6, 1), ("c", 6, 10), ("q", 7, 0), ("q", 7, 1),
("c", 11, 14), ("c", 7), ("c", 15),
)


def grid_kernel(columns, raw, out, left, panels, acc, pure, final, keep_lanes, load_sem,
                left_send, left_recv, panel_send, panel_recv, end_send, end_recv):
    band, block = raw.shape[0], raw.shape[1]
    slab = block // 2
    rank, y = lax.axis_index("rows"), lax.axis_index("inner")
    core, x, low, high = rank % 2, (rank // 2) % 2, (rank // 4) % 2, rank // 8
    other_y = 1 - y

    def flip(bit, by):
        return 1 - bit if by else bit

    def row_at(core_by, x_by, low_by, high_by):
        return 8 * flip(high, high_by) + 4 * flip(low, low_by) + 2 * flip(x, x_by) + flip(core, core_by)

    group_rows = [row_at(0, x_by, 0, high_by) for x_by, high_by in GROUP]
    at_y = {"rows": rank, "inner": other_y}
    at_core = {"rows": row_at(1, 0, 0, 0), "inner": y}
    at_x = {"rows": group_rows[1], "inner": y}
    at_near = {"rows": row_at(0, 0, 1, 0), "inner": y}
    at_far = {"rows": group_rows[2], "inner": y}
    at_xy = {"rows": group_rows[1], "inner": other_y}
    at_far_y = {"rows": group_rows[2], "inner": other_y}
    at_far_x = {"rows": group_rows[3], "inner": y}
    at_far_xy = {"rows": group_rows[3], "inner": other_y}
    everyone = (at_y, at_core, at_x, at_near, at_far, at_xy, at_far_y, at_far_x, at_far_xy)

    barrier = pltpu.get_barrier_semaphore()
    for device in everyone:
        pl.semaphore_signal(barrier, inc=1, device_id=device, device_id_type=MESH)

    loads = []
    for slot in range(band):
        column = (rank + slot + band // 2) % band
        load = pltpu.make_async_copy(raw.at[slot], left.at[0, column], load_sem.at[slot])
        load.start()
        loads.append(load)

    sent = []

    def remote(source, target, send_sem, recv_sem, device):
        return pltpu.make_async_remote_copy(
            src_ref=source, dst_ref=target, send_sem=send_sem, recv_sem=recv_sem, device_id=device, device_id_type=MESH
        )

    def only(wanted, act):
        if wanted is None:
            act()
        else:
            pl.when(wanted)(act)

    def go(copy, wanted=None):
        only(wanted, copy.start)
        sent.append((copy, wanted))

    def column_of(high_by, x_by, y_by, part):
        return 2 * (4 * flip(high, high_by) + 2 * flip(x, x_by) + flip(y, y_by)) + part

    mine = column_of(0, 0, 0, 0)

    def is_read(row, inner_row, first, count):
        s = (first - row + band + band // 2) % band
        a = (inner_row - row + band + band // 2) % band
        return (s + count > band) | ((a - s <= band // 2 - 1 + count) & (s - a <= band // 2 - 1))

    def read_by(which, at, flow, y_by):
        row = group_rows[which]
        if flow == "y":
            return is_read(row, at, column_of(0, 0, 1, 0), 2)
        if y_by:
            return is_read(row, at, column_of(0, 1, 0, 0), 2)
        return is_read(row, at, 2 * (4 * high + 2 * (1 - x)), 4)

    def is_live(row, slot):
        target = (row + slot + band // 2) % band
        found = columns[row, 0] == target
        for at in range(1, columns.shape[1]):
            found = found | (columns[row, at] == target)
        return jnp.where(found, 1, 0)

    def send_left(flow, source, target, device, at, wanted):
        go(remote(left.at[source, at], left.at[target, at], left_send.at[flow, at], left_recv.at[target, at], device), wanted)

    def to_x(source, high_by, x_by, y_by, part):
        at = column_of(high_by, x_by, y_by, part)
        panel = (high_by, x_by, y_by) == (0, 1, 0)
        wanted = None if panel else read_by(source, at, "x", y_by)
        send_left(1 if source == 0 else 2, source, source + 1, at_x, at, wanted)

    def by_x(which, high_by, x_by, y_by):
        return y_by == 0 or (which == 1 and (high_by, 1 - x_by) in EXTRA)

    done = set()

    def take(which, high_by, x_by, y_by, part):
        key = ("left", which, high_by, x_by, y_by, part)
        if key in done:
            return
        done.add(key)
        at = column_of(high_by, x_by, y_by, part)
        ref = left.at[which, at]
        copy = remote(ref, ref, left_send.at[0, at], left_recv.at[which, at], at_y)
        wanted = None
        if y_by:
            wanted = is_read(group_rows[which], at, mine, 2)
        elif which != 2 and (high_by, x_by) != (0, 0):
            wanted = is_read(group_rows[which], at, 2 * (4 * high + 2 * x), 4)
        only(wanted, copy.wait_recv)
        if y_by:
            return
        if (high_by, x_by) == (0, 0):
            own_panel(which, part)
        if which == 2 and fars:
            to_far(*fars.pop(0))
        if which == 2:
            to_x(2, high_by, x_by, 0, part)
        if not (which == 1 and (high_by, 1 - x_by) in EXTRA):
            send_left(2 + which, which, which, at_y, at, read_by(which, at, "y", 0))

    def send_panel(product, source, target, part, device):
        own = product == 0 and source < 4
        ref = left.at[source, mine + part] if own else panels.at[product, source, part]
        go(remote(ref, panels.at[product, target, part], panel_send.at[product, source, target // 8, part],
                  panel_recv.at[product, target, part], device))

    def share(product, which, part):
        send_panel(product, which, 4 + which, part, at_near)
        send_panel(product, which, 8 + which, part, at_core)

    def take_panel(product, source, part):
        key = ("panel", product, source, part)
        if key in done:
            return
        done.add(key)
        ref = panels.at[product, source, part]
        remote(ref, ref, panel_send.at[product, 0, 0, 0], panel_recv.at[product, source, part], at_core).wait_recv()
        if source < 8:
            send_panel(product, source, 8 + source, part, at_core)

    def own_panel(which, part):
        panels[0, which, part] = left[which, mine + part]
        share(0, which, part)

    def apart(a, b):
        return a + b - 2 * a * b

    def source_of(row):
        return (8 * apart(row % 2, core) + 4 * apart((row // 4) % 2, low)
                + 2 * apart(row // 8, high) + apart((row // 2) % 2, x))

    def row_of(source):
        return (8 * apart((source // 2) % 2, high) + 4 * apart((source // 4) % 2, low)
                + 2 * apart(source % 2, x) + apart(source // 8, core))

    def mac(product, which, inner_row, source, part):
        row = group_rows[which]
        valid = is_read(row, inner_row, mine + part, 1)
        term = jnp.dot(left[which, inner_row], panels[product, source, part], preferred_element_type=jnp.float32)
        acc[product, which, part] += jnp.where(valid, term, 0.0)

    def take_row(which):
        for high_by in range(2 if which else 0):
            for x_by in range(2):
                for y_by in range(2):
                    for part in range(2):
                        take(which, high_by, x_by, y_by, part)

    def square_macs(which):
        def body(n, carry):
            for step in range(2):
                inner_row = 2 * n + step
                for part in range(2):
                    mac(0, which, inner_row, source_of(inner_row), part)
            return carry

        lax.fori_loop(0, band // 2, body, 0)

    def cube_macs(*sources):
        for which in range(4):
            take_row(which)
        for source in sources:
            if source < 4:
                assert source in done
                continue
            for part in range(2):
                take_panel(1, source, part)

        def body(n, carry):
            source = sources[0] + (sources[1] - sources[0]) * n if len(sources) > 1 else sources[0]
            for which in range(4):
                for part in range(2):
                    mac(1, which, row_of(source), source, part)
            return carry

        lax.fori_loop(0, len(sources), body, 0)

    def masked(product, which, part):
        keep = keep_lanes[2 * which + part : 2 * which + part + 1] > 0
        return jnp.where(keep, acc[product, which, part], 0.0)

    def square(which):
        for source in range(1, 4):
            for part in range(2):
                take(source, 0, 0, 0, part)
        for source in range(4, 16):
            for part in range(2):
                take_panel(0, source, part)
        take_row(which)
        square_macs(which)
        done.add(which)
        for part in range(2):
            panels[1, which, part] = masked(0, which, part).astype(panels.dtype)
            share(1, which, part)

    def mask_slot(slot, carry):
        column = (rank + slot + band // 2) % band
        keep = jnp.full((1, block), is_live(rank, slot)) > 0
        value = left[0, column]
        left[0, column] = jnp.where(keep, value, jnp.zeros_like(value))
        return carry

    for load in loads:
        load.wait()
    lax.fori_loop(0, band, mask_slot, 0)
    pl.semaphore_wait(barrier, len(everyone))

    def to_far(high_by, x_by, part):
        at = column_of(high_by, x_by, 0, part)
        send_left(0, 0, 2, at_far, at, None)

    fars = [(high_by, x_by, part) for high_by, x_by in ((1, 1), (1, 0), (0, 1), (0, 0)) for part in range(2)]
    for _ in range(WINDOW):
        to_far(*fars.pop(0))
    for part in range(2):
        to_x(0, 0, 1, 0, part)
        own_panel(0, part)
    for which in range(4):
        for part in range(2):
            row = group_rows[which]
            live = is_live(row, (mine + part - row + band + band // 2) % band)
            at = 2 * which + part
            keep_lanes[at : at + 1] = jnp.full((1, block), live)
    acc[...] = jnp.zeros_like(acc)

    acts = {"x": lambda a, b, w, t: to_x(0, a, b, w, t), "l": take, "p": lambda s, t: take_panel(0, s, t),
            "q": lambda s, t: take_panel(1, s, t), "s": square, "c": cube_macs}
    for name, *numbers in ORDER:
        acts[name](*numbers)

    here = pl.ds(pl.multiple_of(y * slab, slab), slab)
    there = pl.ds(pl.multiple_of(other_y * slab, slab), slab)

    def end(which, half, device):
        at = 2 * which + half
        rows = there if half else here
        go(remote(pure.at[which, :, rows], final.at[pl.ds(mine, 2)], end_send.at[at], end_recv.at[at], device))

    ends = {0: ((1, at_y),), 1: ((1, at_xy), (0, at_x)), 2: ((1, at_far_y), (0, at_far)), 3: ((1, at_far_xy), (0, at_far_x))}
    for which in (3, 2, 1, 0):
        for part in range(2):
            total = 3.0 * panels[1, which, part].astype(jnp.float32) - 2.0 * masked(1, which, part)
            pure[which, part] = total.astype(pure.dtype)
        for half, device in ends[which]:
            end(which, half, device)

    def place(value, column):
        out[(column - rank + band + band // 2) % band] = value

    for part in range(2):
        place(pure[0, part, here], mine + part)
    for which in range(4):
        for half, _ in ends[which]:
            x_by, high_by = GROUP[which]
            at = column_of(high_by, x_by, half, 0)
            ref = final.at[pl.ds(at, 2)]
            remote(ref, ref, end_send.at[0], end_recv.at[2 * which + half], at_y).wait_recv()
            for part in range(2):
                place(final[at + part], at + part)
    for copy, wanted in sent:
        only(wanted, copy.wait_send)


def on_grid(blocks, columns):
    _, band, block, _ = blocks.shape
    vmem = pl.BlockSpec(memory_space=pltpu.VMEM)
    dma = pltpu.SemaphoreType.DMA
    result = pl.pallas_call(
        grid_kernel,
        out_shape=jax.ShapeDtypeStruct((band, block // 2, block), blocks.dtype),
        in_specs=[pl.BlockSpec(memory_space=pltpu.SMEM), pl.BlockSpec(memory_space=pl.ANY)],
        out_specs=vmem,
        scratch_shapes=[
            pltpu.VMEM((4, band, block, block), blocks.dtype),
            pltpu.VMEM((2, 16, 2, block, block), blocks.dtype),
            pltpu.VMEM((2, 4, 2, block, block), jnp.float32),
            pltpu.VMEM((4, 2, block, block), blocks.dtype),
            pltpu.VMEM((band, block // 2, block), blocks.dtype),
            pltpu.VMEM((8, block), jnp.int32),
            dma((16,)), dma((6, 16)), dma((4, 16)), dma((2, 8, 2, 2)), dma((2, 16, 2)), dma((8,)), dma((8,)),
        ],
        compiler_params=pltpu.CompilerParams(
            collective_id=0, has_side_effects=True, vmem_limit_bytes=60 * 1024 * 1024
        ),
    )(columns, blocks[0])
    return result[None].astype(jnp.float32)


def from_behind(value, axis, steps):
    count = lax.axis_size(axis)
    pairs = [(source, (source + steps) % count) for source in range(count)]
    return lax.ppermute(value, axis, pairs)


def live_table(columns):
    nrows, band_width = columns.shape
    half_band = band_width // 2
    row_ids = jnp.arange(nrows, dtype=jnp.int32)
    target = (
        row_ids[:, None] + jnp.arange(band_width, dtype=jnp.int32)[None, :] - half_band
    ) % nrows
    return jnp.any(columns[:, None, :] == target[:, :, None], axis=2)


def slot_shift(piece, delta):
    band_width = piece.shape[1]
    if delta >= 0:
        return jnp.concatenate([piece[:, delta:], jnp.zeros_like(piece[:, :delta])], axis=1)
    return jnp.concatenate(
        [jnp.zeros_like(piece[:, :-delta]), piece[:, : band_width + delta]], axis=1
    )


def fetch_band(row_slab, below, above, block_rows, second):
    band_width = row_slab.shape[1]
    pieces = []
    for offset in range(-below, above + 1):
        if offset == 0:
            pieces.append(row_slab)
            continue
        trimmed = (abs(offset) - 1) * block_rows + 1
        if offset > 0:
            outgoing = row_slab[:, : band_width - trimmed]
        else:
            outgoing = row_slab[:, trimmed:]
        if second:
            incoming = from_behind(outgoing, "rows", -offset)
        else:
            incoming = from_behind(outgoing, "rows", -offset)
        filler = jnp.zeros_like(row_slab[:, :trimmed])
        if offset > 0:
            pieces.append(jnp.concatenate([incoming, filler], axis=1))
        else:
            pieces.append(jnp.concatenate([filler, incoming], axis=1))
    return jnp.concatenate(pieces, axis=0)


def merge_groups(totals):
    rounded = lax.optimization_barrier(totals.astype(jnp.bfloat16))
    return jnp.sum(rounded.astype(jnp.float32), axis=0)


def dense_terms(left, window, window_base, groups):
    block_rows, band_width, block_size, inner_width = left.shape
    out_width = window.shape[3]
    half_band = band_width // 2
    group_width = inner_width // groups
    stacked = jnp.stack(
        [
            slot_shift(
                window[window_base + offset : window_base + offset + block_rows], half_band - offset
            )
            for offset in range(band_width)
        ],
        axis=1,
    )
    left_groups = left.reshape(block_rows, band_width, block_size, groups, group_width)
    right_groups = stacked.reshape(
        block_rows, band_width, band_width, groups, group_width, out_width
    )
    totals = jnp.einsum(
        "ramcq,rascqn->crsmn", left_groups, right_groups, preferred_element_type=jnp.float32
    )
    return merge_groups(totals)


def band_terms(left, window, window_base, groups):
    return dense_terms(left, window, window_base, groups)


def per_device(blocks, columns):
    block_rows, band_width, block_size, _ = blocks.shape
    half_band = band_width // 2
    inner_count = lax.axis_size("inner")
    slab_width = block_size // inner_count
    inner_index = lax.axis_index("inner")
    row_owner = lax.axis_index("rows")
    live_own = lax.dynamic_slice_in_dim(live_table(columns), row_owner * block_rows, block_rows, 0)
    live_slots = live_own[:, :, None, None]
    masked = jnp.where(live_slots, blocks, jnp.zeros_like(blocks))
    below = -(-half_band // block_rows)
    above = -(-(half_band - 1) // block_rows)
    window_base = below * block_rows - half_band
    row_slab = lax.dynamic_slice_in_dim(masked, inner_index * slab_width, slab_width, 3)
    window = fetch_band(row_slab, below, above, block_rows, False)
    square = band_terms(masked, window, window_base, inner_count)
    square = jnp.where(live_slots, square, jnp.float32(0.0)).astype(jnp.bfloat16)
    second_window = fetch_band(square, below, above, block_rows, True)
    cubed = band_terms(masked, second_window, window_base, inner_count)
    cubed = jnp.where(live_slots, cubed, jnp.float32(0.0))
    column_slabs = 3.0 * square.astype(jnp.float32) - 2.0 * cubed
    return lax.all_to_all(
        column_slabs.astype(jnp.bfloat16), "inner", split_axis=2, concat_axis=3, tiled=True
    ).astype(column_slabs.dtype)


def solution(mesh):
    in_specs = (P("rows", None, None, None), P())
    out_specs = P("rows", None, "inner", None)

    def step(blocks, columns):
        plain = mesh.shape["rows"] == 16 and mesh.shape["inner"] == 2
        if plain and blocks.shape[:2] == (16, 16) and blocks.shape[2] % 256 == 0:
            chosen = on_grid
        else:
            chosen = per_device
        return jax.shard_map(chosen, mesh=mesh, in_specs=in_specs, out_specs=out_specs, check_vma=False)(
            blocks, columns
        )

    return step
```

time: 127 us -> 118 us (0.929)
  Pallas kernels: 124 us -> 115 us
    pallas_call x1, Pallas kernels: 124 us -> 115 us  [on_grid(): pl.pallas_call(grid_kernel, out_shape=jax.ShapeDtypeStruct((band, block /...]
where the time goes in v1:
time: 118 us
  Pallas kernels  115 us (97%)
  other arithmetic  2.77 us (2%)
    pallas_call x1, Pallas kernels, on_grid(): pl.pallas_call(grid_kernel, out_shape=jax.ShapeDtypeStruct((band, block /...  115 us
    convert_element_type x1, other arithmetic, on_grid(): return result[None].astype(jnp.float32)  2.77 us

profile of v1, /device:TPU:0, one launch (start us, length us, event | category | flops | bytes accessed | tf_op | source)
XLA Modules:
  0.0 117.9 jit_solution(16661616841408986582)
XLA Ops:
  0.0 115.2 %shard_map.28 = bf16[16,128,256]{2,1,0:T(8,128)(2,1)} custom-call(s32[16,16]{1,0:T(8,128)} %columns.1, bf16[16,256,256]{2,1,0:T(8,128)(2,1)} %bitcast.4), custom_call_target="tpu_custom_call" | custom-call | tf_op jit(solution)/shard_map/pallas_call | solution.py:323
  115.2 2.8 %bitcast_convert_fusion = f32[1,16,128,256]{3,2,1,0:T(8,128)} fusion(bf16[16,128,256]{2,1,0:T(8,128)(2,1)} %shard_map.28), kind=kLoop, calls=%fused_computation | loop fusion | flops 524288 | bytes 3145728 | tf_op jit(solution)/shard_map/convert_element_type | solution.py:341

commit v2 on v1

--- a/solution.py
+++ b/solution.py
@@ -10,28 +10,25 @@
 MESH = pl.DeviceIdType.MESH
 
 WINDOW = 3
-EXTRA = ((0, 0),)
+EXTRA = ((1, 0),)
 GROUP = ((0, 0), (1, 0), (0, 1), (1, 1))
 ORDER = (
-    ("x", 1, 1, 0, 0), ("x", 1, 1, 0, 1), ("l", 1, 0, 0, 0, 0), ("l", 1, 0, 0, 0, 1), ("p", 4, 0),
-("p", 4, 1), ("x", 0, 0, 0, 0), ("x", 0, 0, 0, 1), ("l", 2, 0, 1, 0, 0), ("l", 2, 0, 1, 0, 1),
-("x", 1, 0, 0, 0), ("x", 1, 0, 0, 1), ("l", 1, 1, 0, 0, 0), ("l", 1, 1, 0, 0, 1), ("p", 5, 0), ("p", 5, 1),
-("l", 3, 0, 0, 0, 0), ("l", 3, 0, 0, 0, 1), ("l", 2, 0, 0, 0, 0), ("l", 2, 0, 0, 0, 1),
-("l", 1, 0, 1, 0, 0), ("l", 1, 0, 1, 0, 1), ("x", 0, 0, 1, 0), ("x", 0, 0, 1, 1), ("l", 1, 1, 1, 0, 0),
-("l", 1, 1, 1, 0, 1), ("p", 7, 0), ("p", 7, 1), ("l", 3, 0, 1, 0, 0), ("l", 3, 0, 1, 0, 1), ("p", 6, 0),
-("p", 6, 1), ("l", 2, 1, 1, 0, 0), ("l", 2, 1, 1, 0, 1), ("p", 8, 0), ("p", 8, 1), ("p", 9, 0), ("p", 9, 1),
-("p", 10, 0), ("p", 10, 1), ("p", 11, 0), ("p", 11, 1), ("p", 12, 0), ("p", 12, 1), ("p", 13, 0),
-("p", 13, 1), ("p", 14, 0), ("p", 14, 1), ("p", 15, 0), ("p", 15, 1), ("s", 0), ("l", 3, 1, 0, 0, 0),
-("l", 3, 1, 0, 0, 1), ("l", 1, 0, 0, 1, 0), ("l", 1, 0, 0, 1, 1), ("l", 1, 1, 0, 1, 0),
-("l", 1, 1, 0, 1, 1), ("l", 1, 0, 1, 1, 0), ("l", 1, 0, 1, 1, 1), ("l", 1, 1, 1, 1, 0),
-("l", 1, 1, 1, 1, 1), ("s", 1), ("l", 2, 1, 0, 0, 0), ("l", 2, 1, 0, 0, 1), ("q", 4, 0), ("q", 4, 1),
-("l", 3, 1, 1, 0, 0), ("l", 3, 1, 1, 0, 1), ("l", 2, 0, 1, 1, 0), ("l", 2, 0, 1, 1, 1),
-("l", 2, 0, 0, 1, 0), ("l", 2, 0, 0, 1, 1), ("l", 2, 1, 1, 1, 0), ("l", 2, 1, 1, 1, 1),
-("l", 2, 1, 0, 1, 0), ("l", 2, 1, 0, 1, 1), ("s", 2), ("q", 5, 0), ("q", 5, 1), ("l", 3, 0, 0, 1, 0),
-("l", 3, 0, 0, 1, 1), ("l", 3, 0, 1, 1, 0), ("l", 3, 0, 1, 1, 1), ("l", 3, 1, 0, 1, 0),
-("l", 3, 1, 0, 1, 1), ("l", 3, 1, 1, 1, 0), ("l", 3, 1, 1, 1, 1), ("s", 3), ("c", 0, 1), ("c", 2, 3),
-("c", 4, 5), ("c", 8, 9), ("c", 12, 13), ("q", 6, 0), ("q", 6, 1), ("c", 6, 10), ("q", 7, 0), ("q", 7, 1),
-("c", 11, 14), ("c", 7), ("c", 15),
+    ("x", 1, 1, 0, 0), ("x", 1, 1, 0, 1), ("l", 1, 0, 0, 0, 0), ("n", 1, 0), ("l", 1, 0, 0, 0, 1),
+("l", 2, 0, 1, 0, 0), ("n", 0, 1), ("x", 0, 0, 0, 0), ("l", 1, 1, 0, 0, 0), ("l", 1, 1, 0, 0, 1),
+("l", 2, 0, 1, 0, 1), ("x", 0, 0, 0, 1), ("p", 4, 0), ("l", 3, 0, 0, 0, 0), ("n", 3, 0), ("x", 1, 0, 0, 0),
+("l", 2, 0, 0, 0, 0), ("n", 2, 0), ("l", 1, 0, 1, 0, 0), ("p", 5, 0), ("l", 3, 0, 0, 0, 1),
+("x", 1, 0, 0, 1), ("n", 1, 1), ("l", 1, 0, 1, 0, 1), ("l", 2, 0, 0, 0, 1), ("n", 3, 1), ("n", 2, 1),
+("l", 3, 0, 1, 0, 0), ("x", 1, 0, 1, 0), ("x", 1, 0, 1, 1), ("l", 1, 1, 1, 0, 0), ("p", 7, 0),
+("l", 2, 1, 1, 0, 0), ("p", 6, 0), ("l", 3, 0, 1, 0, 1), ("l", 1, 1, 1, 0, 1), ("l", 2, 1, 1, 0, 1),
+("s", 0, 0, 0), ("l", 3, 1, 0, 0, 0), ("p", 4, 1), ("p", 5, 1), ("l", 2, 1, 0, 0, 0), ("m", 1, 0, 0, 4),
+("m", 2, 0, 0, 4), ("s", 1, 0, 4), ("l", 3, 1, 0, 0, 1), ("p", 7, 1), ("l", 2, 1, 0, 0, 1),
+("m", 3, 0, 0, 4), ("p", 6, 1), ("s", 0, 1, 0), ("l", 3, 1, 1, 0, 0), ("m", 1, 1, 0, 4), ("s", 1, 1, 4),
+("m", 2, 1, 0, 4), ("l", 3, 1, 1, 0, 1), ("m", 3, 1, 0, 4), ("s", 2, 0, 4), ("q", 4, 0), ("s", 3, 0, 4),
+("q", 5, 0), ("c", 0, 0, 1, 4), ("s", 2, 1, 4), ("q", 6, 0), ("s", 3, 1, 4), ("c", 0, 8, 1, 2),
+("c", 0, 4, 1, 2), ("c", 0, 12, 1, 2), ("c", 0, 10, 1, 2), ("q", 7, 0), ("c", 0, 6, 8, 2),
+("c", 0, 7, 8, 2), ("e", 0), ("q", 4, 1), ("q", 5, 1), ("c", 1, 0, 1, 4), ("c", 1, 8, 1, 2),
+("c", 1, 4, 1, 2), ("c", 1, 12, 1, 2), ("q", 6, 1), ("c", 1, 10, 1, 2), ("c", 1, 6, 8, 2), ("q", 7, 1),
+("c", 1, 7, 8, 2), ("e", 1),
 )
 
 
@@ -42,6 +39,9 @@
     rank, y = lax.axis_index("rows"), lax.axis_index("inner")
     core, x, low, high = rank % 2, (rank // 2) % 2, (rank // 4) % 2, rank // 8
     other_y = 1 - y
+
+    def wrap(value):
+        return lax.rem(value, band)
 
     def flip(bit, by):
         return 1 - bit if by else bit
@@ -67,7 +67,7 @@
 
     loads = []
     for slot in range(band):
-        column = (rank + slot + band // 2) % band
+        column = wrap(rank + slot + band // 2)
         load = pltpu.make_async_copy(raw.at[slot], left.at[0, column], load_sem.at[slot])
         load.start()
         loads.append(load)
@@ -95,8 +95,8 @@
     mine = column_of(0, 0, 0, 0)
 
     def is_read(row, inner_row, first, count):
-        s = (first - row + band + band // 2) % band
-        a = (inner_row - row + band + band // 2) % band
+        s = wrap(first - row + band + band // 2)
+        a = wrap(inner_row - row + band + band // 2)
         return (s + count > band) | ((a - s <= band // 2 - 1 + count) & (s - a <= band // 2 - 1))
 
     def read_by(which, at, flow, y_by):
@@ -108,7 +108,7 @@
         return is_read(row, at, 2 * (4 * high + 2 * (1 - x)), 4)
 
     def is_live(row, slot):
-        target = (row + slot + band // 2) % band
+        target = wrap(row + slot + band // 2)
         found = columns[row, 0] == target
         for at in range(1, columns.shape[1]):
             found = found | (columns[row, at] == target)
@@ -145,7 +145,7 @@
         if y_by:
             return
         if (high_by, x_by) == (0, 0):
-            own_panel(which, part)
+            panels[0, which, part] = left[which, mine + part]
         if which == 2 and fars:
             to_far(*fars.pop(0))
         if which == 2:
@@ -174,7 +174,10 @@
             send_panel(product, source, 8 + source, part, at_core)
 
     def own_panel(which, part):
-        panels[0, which, part] = left[which, mine + part]
+        if which:
+            take(which, 0, 0, 0, part)
+        else:
+            panels[0, which, part] = left[which, mine + part]
         share(0, which, part)
 
     def apart(a, b):
@@ -188,11 +191,15 @@
         return (8 * apart((source // 2) % 2, high) + 4 * apart((source // 4) % 2, low)
                 + 2 * apart(source % 2, x) + apart(source // 8, core))
 
-    def mac(product, which, inner_row, source, part):
+    def mac(product, which, part, terms):
         row = group_rows[which]
-        valid = is_read(row, inner_row, mine + part, 1)
-        term = jnp.dot(left[which, inner_row], panels[product, source, part], preferred_element_type=jnp.float32)
-        acc[product, which, part] += jnp.where(valid, term, 0.0)
+        total = None
+        for inner_row, source in terms:
+            valid = is_read(row, inner_row, mine + part, 1)
+            term = jnp.dot(left[which, inner_row], panels[product, source, part], preferred_element_type=jnp.float32)
+            term = jnp.where(valid, term, 0.0)
+            total = term if total is None else total + term
+        acc[product, which, part] += total
 
     def take_row(which):
         for high_by in range(2 if which else 0):
@@ -201,55 +208,60 @@
                     for part in range(2):
                         take(which, high_by, x_by, y_by, part)
 
-    def square_macs(which):
+    def square_macs(which, part, first, count):
+        for high_by in range(first // 4, (first + count) // 4):
+            for x_by in range(2):
+                for y_by in range(2):
+                    for at in range(2):
+                        if which:
+                            take(which, high_by, x_by, y_by, at)
+        for source in range(1, 4):
+            take(source, 0, 0, 0, part)
+        for source in range(4, 16):
+            take_panel(0, source, part)
+
         def body(n, carry):
-            for step in range(2):
-                inner_row = 2 * n + step
-                for part in range(2):
-                    mac(0, which, inner_row, source_of(inner_row), part)
+            high_by, x_by, y_by = n // 4, lax.rem(n // 2, 2), lax.rem(n, 2)
+            inner_row = 2 * (4 * apart(high, high_by) + 2 * apart(x, x_by) + apart(y, y_by))
+            mac(0, which, part, [(inner_row + step, source_of(inner_row + step)) for step in range(2)])
             return carry
 
-        lax.fori_loop(0, band // 2, body, 0)
-
-    def cube_macs(*sources):
+        lax.fori_loop(first, first + count, body, 0)
+        assert (which, part) not in done
+        done.add((which, part, first + count))
+
+    def cube_macs(part, first, stride, count):
         for which in range(4):
             take_row(which)
-        for source in sources:
+        for n in range(count):
+            source = first + n * stride
+            done.add(("cube", source, part))
             if source < 4:
-                assert source in done
-                continue
-            for part in range(2):
+                assert (source, part) in done
+            else:
                 take_panel(1, source, part)
 
         def body(n, carry):
-            source = sources[0] + (sources[1] - sources[0]) * n if len(sources) > 1 else sources[0]
+            sources = [first + (2 * n + step) * stride for step in range(2)]
             for which in range(4):
-                for part in range(2):
-                    mac(1, which, row_of(source), source, part)
+                mac(1, which, part, [(row_of(source), source) for source in sources])
             return carry
 
-        lax.fori_loop(0, len(sources), body, 0)
+        lax.fori_loop(0, count // 2, body, 0)
 
     def masked(product, which, part):
         keep = keep_lanes[2 * which + part : 2 * which + part + 1] > 0
         return jnp.where(keep, acc[product, which, part], 0.0)
 
-    def square(which):
-        for source in range(1, 4):
-            for part in range(2):
-                take(source, 0, 0, 0, part)
-        for source in range(4, 16):
-            for part in range(2):
-                take_panel(0, source, part)
-        take_row(which)
-        square_macs(which)
-        done.add(which)
-        for part in range(2):
-            panels[1, which, part] = masked(0, which, part).astype(panels.dtype)
-            share(1, which, part)
+    def square(which, part, first):
+        assert first == 0 or (which, part, first) in done
+        square_macs(which, part, first, 8 - first)
+        done.add((which, part))
+        panels[1, which, part] = masked(0, which, part).astype(panels.dtype)
+        share(1, which, part)
 
     def mask_slot(slot, carry):
-        column = (rank + slot + band // 2) % band
+        column = wrap(rank + slot + band // 2)
         keep = jnp.full((1, block), is_live(rank, slot)) > 0
         value = left[0, column]
         left[0, column] = jnp.where(keep, value, jnp.zeros_like(value))
@@ -269,49 +281,48 @@
         to_far(*fars.pop(0))
     for part in range(2):
         to_x(0, 0, 1, 0, part)
-        own_panel(0, part)
+    own_panel(0, 0)
     for which in range(4):
         for part in range(2):
             row = group_rows[which]
-            live = is_live(row, (mine + part - row + band + band // 2) % band)
+            live = is_live(row, wrap(mine + part - row + band + band // 2))
             at = 2 * which + part
             keep_lanes[at : at + 1] = jnp.full((1, block), live)
     acc[...] = jnp.zeros_like(acc)
 
-    acts = {"x": lambda a, b, w, t: to_x(0, a, b, w, t), "l": take, "p": lambda s, t: take_panel(0, s, t),
-            "q": lambda s, t: take_panel(1, s, t), "s": square, "c": cube_macs}
+    here = pl.ds(pl.multiple_of(y * slab, slab), slab)
+    there = pl.ds(pl.multiple_of(other_y * slab, slab), slab)
+    ends = {0: ((1, at_y),), 1: ((1, at_xy), (0, at_x)), 2: ((1, at_far_y), (0, at_far)), 3: ((1, at_far_xy), (0, at_far_x))}
+
+    def finish(part):
+        assert all(("cube", source, part) in done for source in range(16))
+        for which in (3, 2, 1, 0):
+            total = 3.0 * panels[1, which, part].astype(jnp.float32) - 2.0 * masked(1, which, part)
+            pure[which, part] = total.astype(pure.dtype)
+            for half, device in ends[which]:
+                at = 2 * which + half
+                rows = there if half else here
+                go(remote(pure.at[which, part, rows], final.at[mine + part], end_send.at[at, part],
+                          end_recv.at[at, part], device))
+
+    acts = {"x": lambda a, b, w, t: to_x(0, a, b, w, t), "l": take, "n": own_panel,
+            "p": lambda s, t: take_panel(0, s, t), "q": lambda s, t: take_panel(1, s, t),
+            "m": square_macs, "s": square, "c": cube_macs, "e": finish}
     for name, *numbers in ORDER:
         acts[name](*numbers)
 
-    here = pl.ds(pl.multiple_of(y * slab, slab), slab)
-    there = pl.ds(pl.multiple_of(other_y * slab, slab), slab)
-
-    def end(which, half, device):
-        at = 2 * which + half
-        rows = there if half else here
-        go(remote(pure.at[which, :, rows], final.at[pl.ds(mine, 2)], end_send.at[at], end_recv.at[at], device))
-
-    ends = {0: ((1, at_y),), 1: ((1, at_xy), (0, at_x)), 2: ((1, at_far_y), (0, at_far)), 3: ((1, at_far_xy), (0, at_far_x))}
-    for which in (3, 2, 1, 0):
-        for part in range(2):
-            total = 3.0 * panels[1, which, part].astype(jnp.float32) - 2.0 * masked(1, which, part)
-            pure[which, part] = total.astype(pure.dtype)
-        for half, device in ends[which]:
-            end(which, half, device)
-
     def place(value, column):
-        out[(column - rank + band + band // 2) % band] = value
+        out[wrap(column - rank + band + band // 2)] = value
 
     for part in range(2):
         place(pure[0, part, here], mine + part)
-    for which in range(4):
-        for half, _ in ends[which]:
-            x_by, high_by = GROUP[which]
-            at = column_of(high_by, x_by, half, 0)
-            ref = final.at[pl.ds(at, 2)]
-            remote(ref, ref, end_send.at[0], end_recv.at[2 * which + half], at_y).wait_recv()
-            for part in range(2):
-                place(final[at + part], at + part)
+        for which in range(4):
+            for half, _ in ends[which]:
+                x_by, high_by = GROUP[which]
+                at = column_of(high_by, x_by, half, part)
+                ref = final.at[at]
+                remote(ref, ref, end_send.at[0, 0], end_recv.at[2 * which + half, part], at_y).wait_recv()
+                place(final[at], at)
     for copy, wanted in sent:
         only(wanted, copy.wait_send)
 
@@ -332,7 +343,7 @@
             pltpu.VMEM((4, 2, block, block), blocks.dtype),
             pltpu.VMEM((band, block // 2, block), blocks.dtype),
             pltpu.VMEM((8, block), jnp.int32),
-            dma((16,)), dma((6, 16)), dma((4, 16)), dma((2, 8, 2, 2)), dma((2, 16, 2)), dma((8,)), dma((8,)),
+            dma((16,)), dma((6, 16)), dma((4, 16)), dma((2, 8, 2, 2)), dma((2, 16, 2)), dma((8, 2)), dma((8, 2)),
         ],
         compiler_params=pltpu.CompilerParams(
             collective_id=0, has_side_effects=True, vmem_limit_bytes=60 * 1024 * 1024

time: 118 us -> 109 us (0.924)
  Pallas kernels: 115 us -> 106 us
    pallas_call x1, Pallas kernels: 115 us -> 106 us  [on_grid(): pl.pallas_call(grid_kernel, out_shape=jax.ShapeDtypeStruct((band, block /...]
where the time goes in v2:
time: 109 us
  Pallas kernels  106 us (97%)
  other arithmetic  2.77 us (3%)
    pallas_call x1, Pallas kernels, on_grid(): pl.pallas_call(grid_kernel, out_shape=jax.ShapeDtypeStruct((band, block /...  106 us
    convert_element_type x1, other arithmetic, on_grid(): return result[None].astype(jnp.float32)  2.77 us

profile of v2, /device:TPU:0, one launch (start us, length us, event | category | flops | bytes accessed | tf_op | source)
XLA Modules:
  0.0 108.9 jit_solution(10816190442899475391)
XLA Ops:
  0.0 106.1 %shard_map.28 = bf16[16,128,256]{2,1,0:T(8,128)(2,1)} custom-call(s32[16,16]{1,0:T(8,128)} %columns.1, bf16[16,256,256]{2,1,0:T(8,128)(2,1)} %bitcast.4), custom_call_target="tpu_custom_call" | custom-call | tf_op jit(solution)/shard_map/pallas_call | solution.py:334
  106.1 2.8 %bitcast_convert_fusion = f32[1,16,128,256]{3,2,1,0:T(8,128)} fusion(bf16[16,128,256]{2,1,0:T(8,128)(2,1)} %shard_map.28), kind=kLoop, calls=%fused_computation | loop fusion | flops 524288 | bytes 3145728 | tf_op jit(solution)/shard_map/convert_element_type | solution.py:352

commit v3 on v2

--- a/solution.py
+++ b/solution.py
@@ -9,7 +9,8 @@
 
 MESH = pl.DeviceIdType.MESH
 
-WINDOW = 3
+WINDOW = 2
+DIAGONAL = ((1, 0, 1),)
 EXTRA = ((1, 0),)
 GROUP = ((0, 0), (1, 0), (0, 1), (1, 1))
 ORDER = (
@@ -150,7 +151,10 @@
             to_far(*fars.pop(0))
         if which == 2:
             to_x(2, high_by, x_by, 0, part)
-        if not (which == 1 and (high_by, 1 - x_by) in EXTRA):
+            if (high_by, x_by, part) in DIAGONAL:
+                wanted = is_read(group_rows[2], at, column_of(0, 1, 1, 0), 2)
+                send_left(6, 2, 3, at_xy, at, wanted)
+        if not (which == 1 and (high_by, 1 - x_by) in EXTRA or which == 3 and (high_by, 1 - x_by, part) in DIAGONAL):
             send_left(2 + which, which, which, at_y, at, read_by(which, at, "y", 0))
 
     def send_panel(product, source, target, part, device):
@@ -260,21 +264,31 @@
         panels[1, which, part] = masked(0, which, part).astype(panels.dtype)
         share(1, which, part)
 
-    def mask_slot(slot, carry):
-        column = wrap(rank + slot + band // 2)
-        keep = jnp.full((1, block), is_live(rank, slot)) > 0
+    def mask(column):
+        row_slot = wrap(column - rank + band + band // 2)
+        keep = jnp.full((1, block), is_live(rank, row_slot)) > 0
         value = left[0, column]
         left[0, column] = jnp.where(keep, value, jnp.zeros_like(value))
+
+    def mask_chunk(n, carry):
+        high_by, x_by, y_by = n // 4, lax.rem(n // 2, 2), lax.rem(n, 2)
+        first = 2 * (4 * apart(high, high_by) + 2 * apart(x, x_by) + apart(y, y_by))
+        mask(first)
+        mask(first + 1)
         return carry
+
+    def mask_more():
+        lax.fori_loop(3, 6, mask_chunk, 0)
+        lax.fori_loop(7, 8, mask_chunk, 0)
 
     for load in loads:
         load.wait()
-    lax.fori_loop(0, band, mask_slot, 0)
+    lax.fori_loop(0, 3, mask_chunk, 0)
+    lax.fori_loop(6, 7, mask_chunk, 0)
     pl.semaphore_wait(barrier, len(everyone))
 
     def to_far(high_by, x_by, part):
-        at = column_of(high_by, x_by, 0, part)
-        send_left(0, 0, 2, at_far, at, None)
+        send_left(0, 0, 2, at_far, column_of(high_by, x_by, 0, part), None)
 
     fars = [(high_by, x_by, part) for high_by, x_by in ((1, 1), (1, 0), (0, 1), (0, 0)) for part in range(2)]
     for _ in range(WINDOW):
@@ -282,6 +296,7 @@
     for part in range(2):
         to_x(0, 0, 1, 0, part)
     own_panel(0, 0)
+    mask_more()
     for which in range(4):
         for part in range(2):
             row = group_rows[which]
@@ -311,31 +326,36 @@
     for name, *numbers in ORDER:
         acts[name](*numbers)
 
-    def place(value, column):
-        out[wrap(column - rank + band + band // 2)] = value
+    outs = []
+
+    def put(ref, column):
+        copy = pltpu.make_async_copy(ref, out.at[wrap(column - rank + band + band // 2)], load_sem.at[len(outs)])
+        copy.start()
+        outs.append(copy)
 
     for part in range(2):
-        place(pure[0, part, here], mine + part)
+        put(pure.at[0, part, here], mine + part)
         for which in range(4):
             for half, _ in ends[which]:
                 x_by, high_by = GROUP[which]
                 at = column_of(high_by, x_by, half, part)
                 ref = final.at[at]
                 remote(ref, ref, end_send.at[0, 0], end_recv.at[2 * which + half, part], at_y).wait_recv()
-                place(final[at], at)
+                put(ref, at)
+    for copy in outs:
+        copy.wait()
     for copy, wanted in sent:
         only(wanted, copy.wait_send)
 
 
 def on_grid(blocks, columns):
     _, band, block, _ = blocks.shape
-    vmem = pl.BlockSpec(memory_space=pltpu.VMEM)
     dma = pltpu.SemaphoreType.DMA
     result = pl.pallas_call(
         grid_kernel,
         out_shape=jax.ShapeDtypeStruct((band, block // 2, block), blocks.dtype),
         in_specs=[pl.BlockSpec(memory_space=pltpu.SMEM), pl.BlockSpec(memory_space=pl.ANY)],
-        out_specs=vmem,
+        out_specs=pl.BlockSpec(memory_space=pl.ANY),
         scratch_shapes=[
             pltpu.VMEM((4, band, block, block), blocks.dtype),
             pltpu.VMEM((2, 16, 2, block, block), blocks.dtype),
@@ -343,7 +363,7 @@
             pltpu.VMEM((4, 2, block, block), blocks.dtype),
             pltpu.VMEM((band, block // 2, block), blocks.dtype),
             pltpu.VMEM((8, block), jnp.int32),
-            dma((16,)), dma((6, 16)), dma((4, 16)), dma((2, 8, 2, 2)), dma((2, 16, 2)), dma((8, 2)), dma((8, 2)),
+            dma((16,)), dma((7, 16)), dma((4, 16)), dma((2, 8, 2, 2)), dma((2, 16, 2)), dma((8, 2)), dma((8, 2)),
         ],
         compiler_params=pltpu.CompilerParams(
             collective_id=0, has_side_effects=True, vmem_limit_bytes=60 * 1024 * 1024

time: 109 us -> 106 us (0.972)
  Pallas kernels: 106 us -> 103 us
    pallas_call x1, Pallas kernels: 106 us -> 103 us  [on_grid(): pl.pallas_call(grid_kernel, out_shape=jax.ShapeDtypeStruct((band, block /...]
where the time goes in v3:
time: 106 us
  Pallas kernels  103 us (97%)
  other arithmetic  2.77 us (3%)
    pallas_call x1, Pallas kernels, on_grid(): pl.pallas_call(grid_kernel, out_shape=jax.ShapeDtypeStruct((band, block /...  103 us
    convert_element_type x1, other arithmetic, on_grid(): return result[None].astype(jnp.float32)  2.77 us

profile of v3, /device:TPU:0, one launch (start us, length us, event | category | flops | bytes accessed | tf_op | source)
XLA Modules:
  0.0 105.9 jit_solution(4150117715044165330)
XLA Ops:
  0.0 103.1 %shard_map.28 = bf16[16,128,256]{2,1,0:T(8,128)(2,1)} custom-call(s32[16,16]{1,0:T(8,128)} %columns.1, bf16[16,256,256]{2,1,0:T(8,128)(2,1)} %bitcast.4), custom_call_target="tpu_custom_call" | custom-call | tf_op jit(solution)/shard_map/pallas_call | solution.py:354
  103.1 2.8 %bitcast_convert_fusion = f32[1,16,128,256]{3,2,1,0:T(8,128)} fusion(bf16[16,128,256]{2,1,0:T(8,128)(2,1)} %shard_map.28), kind=kLoop, calls=%fused_computation | loop fusion | flops 524288 | bytes 3145728 | tf_op jit(solution)/shard_map/convert_element_type | solution.py:372

commit v4 on v3

--- a/solution.py
+++ b/solution.py
@@ -14,8 +14,8 @@
 EXTRA = ((1, 0),)
 GROUP = ((0, 0), (1, 0), (0, 1), (1, 1))
 ORDER = (
-    ("x", 1, 1, 0, 0), ("x", 1, 1, 0, 1), ("l", 1, 0, 0, 0, 0), ("n", 1, 0), ("l", 1, 0, 0, 0, 1),
-("l", 2, 0, 1, 0, 0), ("n", 0, 1), ("x", 0, 0, 0, 0), ("l", 1, 1, 0, 0, 0), ("l", 1, 1, 0, 0, 1),
+    ("n", 0, 1), ("x", 1, 1, 0, 0), ("x", 1, 1, 0, 1), ("l", 1, 0, 0, 0, 0), ("n", 1, 0),
+("l", 1, 0, 0, 0, 1), ("l", 2, 0, 1, 0, 0), ("x", 0, 0, 0, 0), ("l", 1, 1, 0, 0, 0), ("l", 1, 1, 0, 0, 1),
 ("l", 2, 0, 1, 0, 1), ("x", 0, 0, 0, 1), ("p", 4, 0), ("l", 3, 0, 0, 0, 0), ("n", 3, 0), ("x", 1, 0, 0, 0),
 ("l", 2, 0, 0, 0, 0), ("n", 2, 0), ("l", 1, 0, 1, 0, 0), ("p", 5, 0), ("l", 3, 0, 0, 0, 1),
 ("x", 1, 0, 0, 1), ("n", 1, 1), ("l", 1, 0, 1, 0, 1), ("l", 2, 0, 0, 0, 1), ("n", 3, 1), ("n", 2, 1),

time: 106 us -> 105 us (level)
    pallas_call x1, Pallas kernels: 103 us -> 102 us  [on_grid(): pl.pallas_call(grid_kernel, out_shape=jax.ShapeDtypeStruct((band, block /...]
where the time goes in v4:
time: 105 us
  Pallas kernels  102 us (97%)
  other arithmetic  2.77 us (3%)
    pallas_call x1, Pallas kernels, on_grid(): pl.pallas_call(grid_kernel, out_shape=jax.ShapeDtypeStruct((band, block /...  102 us
    convert_element_type x1, other arithmetic, on_grid(): return result[None].astype(jnp.float32)  2.77 us

profile of v4, /device:TPU:0, one launch (start us, length us, event | category | flops | bytes accessed | tf_op | source)
XLA Modules:
  0.0 104.8 jit_solution(18398175139823796557)
XLA Ops:
  0.0 102.0 %shard_map.28 = bf16[16,128,256]{2,1,0:T(8,128)(2,1)} custom-call(s32[16,16]{1,0:T(8,128)} %columns.1, bf16[16,256,256]{2,1,0:T(8,128)(2,1)} %bitcast.4), custom_call_target="tpu_custom_call" | custom-call | tf_op jit(solution)/shard_map/pallas_call | solution.py:354
  102.0 2.8 %bitcast_convert_fusion = f32[1,16,128,256]{3,2,1,0:T(8,128)} fusion(bf16[16,128,256]{2,1,0:T(8,128)(2,1)} %shard_map.28), kind=kLoop, calls=%fused_computation | loop fusion | flops 524288 | bytes 3145728 | tf_op jit(solution)/shard_map/convert_element_type | solution.py:372
